TPU v7x, 32 devices: a whole 2x2x4 slice. The times are simulated.
32 devices in a mesh: batch: 16 (over z, y, core), gene: 2 (over x).
Axes of the slice: x: 2, y: 2, z: 4, core: 2. Of those that a mesh axis runs over, the one named last changes fastest.
Arguments:
- umi_counts: int32 [16384, 8192], P('batch', 'gene'), may hold values from 0 to 65535
- cell_donors: int32 [16384], P('batch'), may hold values from 0 to 127
- cell_types: int32 [16384], P('batch'), may hold values from 0 to 23
- live_cells: int32 [16], P('batch'), may hold values from 1 to 1024, 10240 in all
- dosages: int32 [128, 2048], P(None, 'batch'), may hold values from 0 to 2
Outputs:
- scores: bfloat16 [24, 8192, 2048], P(None, ('gene', 'batch'))
All inputs are finite; a program needn't handle non-finite values. No bound on the sum of `live_cells` on one device may be relied on, other than what follows from the above.
Results may differ from a plain program's by a relative error of at most 0.0069.
Values may be sent and summed in bfloat16 or wider, within the bound.
A program may use at most 128 MiB of HBM per device.

v0:
```python
import jax
import jax.numpy as jnp
from jax import lax
from jax.sharding import PartitionSpec as P

TYPES = 24
DONORS = 128


def one_hot_rows(group_ids, total_groups):
    columns = jnp.arange(total_groups, dtype=jnp.int32)
    return (group_ids[:, None] == columns[None, :]).astype(jnp.bfloat16)


def standardize_dosage(block_dosage):
    genotype = block_dosage.astype(jnp.float32)
    centred = genotype - jnp.mean(genotype, axis=0, keepdims=True)
    return (centred * lax.rsqrt(jnp.mean(centred * centred, axis=0, keepdims=True) + 1e-06)).astype(
        jnp.bfloat16
    )


def on_device(umi_counts, cell_donors, cell_types, live_cells, dosages):
    total_groups = TYPES * DONORS
    cell_slots = umi_counts.shape[0]
    genes_block = umi_counts.shape[1]
    batch_count = lax.axis_size("batch")
    genes_local = genes_block // batch_count
    slot_index = jnp.arange(cell_slots, dtype=jnp.int32)
    alive_mask = slot_index < live_cells[0]
    cell_group = jnp.where(alive_mask, cell_types * DONORS + cell_donors, -1)
    rounded = umi_counts.astype(jnp.bfloat16)
    exchanged = lax.all_to_all(rounded, "batch", split_axis=1, concat_axis=0, tiled=True)
    all_groups = lax.all_gather(cell_group, "batch", axis=0, tiled=True)
    block_rows = 4 * cell_slots
    block_turns = batch_count // 4

    def add_block(step_index, totals):
        block_counts = lax.dynamic_slice_in_dim(exchanged, step_index * block_rows, block_rows, 0)
        block_groups = lax.dynamic_slice_in_dim(all_groups, step_index * block_rows, block_rows, 0)
        table = one_hot_rows(block_groups, total_groups)
        return totals + lax.dot_general(
            block_counts, table, (((0,), (0,)), ((), ())), preferred_element_type=jnp.float32
        )

    pseudo = lax.fori_loop(
        0, block_turns, add_block, jnp.zeros((genes_local, total_groups), jnp.float32)
    )
    partial_library = jnp.sum(pseudo, axis=0)
    library = jnp.maximum(lax.psum(partial_library, ("batch", "gene")), 1.0)
    logged = jnp.log1p(10000.0 * pseudo / library[None, :]).reshape(genes_local, TYPES, DONORS)
    centred = logged - jnp.mean(logged, axis=2, keepdims=True)
    standard = (
        centred * lax.rsqrt(jnp.mean(centred * centred, axis=2, keepdims=True) + 1e-06)
    ).astype(jnp.bfloat16)
    standard_rows = jnp.transpose(standard, (1, 0, 2)).reshape(TYPES * genes_local, DONORS)
    factor = DONORS ** (-0.5)
    geno_local = standardize_dosage(dosages)
    geno_piece = lax.all_gather(geno_local, "batch", axis=1, tiled=True)
    product = jnp.dot(standard_rows, geno_piece, preferred_element_type=jnp.float32) * factor
    return product.reshape(TYPES, genes_local, geno_piece.shape[1]).astype(jnp.bfloat16)


def solution(mesh):
    placed = (P("batch", "gene"), P("batch"), P("batch"), P("batch"), P(None, "batch"))
    return jax.shard_map(
        on_device,
        mesh=mesh,
        in_specs=placed,
        out_specs=P(None, ("gene", "batch"), None),
        check_vma=False,
    )
```

profile of v0, /device:TPU:14, one launch (start us, length us, event | category | flops | bytes accessed | tf_op | source)
XLA Modules:
  0.0 357.4 jit_solution(3607183109049914522)
XLA Ops:
  0.0 9.0 %convert_element_type.21 = bf16[1024,4096]{1,0:T(8,128)(2,1)} convert(s32[1024,4096]{1,0:T(8,128)} %param.7) | non-fusion elementwise | flops 4194304 | bytes 25165824 | tf_op jit(solution)/shard_map/convert_element_type | solution.py:32
  9.0 7.4 %copy.16 = bf16[128,16,8,256]{3,2,0,1:T(8,128)(2,1)} copy(bf16[128,16,8,256]{3,2,1,0:T(8,128)(2,1)} %bitcast.19) | data formatting | bytes 16777216 | tf_op jit(solution)/shard_map/all_to_all | solution.py:33
  16.5 0.0 copy-start.2
  16.5 0.0 copy-start.3
  16.5 0.0 copy-start.1
  16.5 6.4 %all-to-all-start = ((bf16[1024,16,256]{2,0,1:T(8,128)(2,1)}), bf16[1024,16,256]{2,0,1:T(8,128)(2,1)}, u32[]{:S(2)}, u32[]{:S(2)}) async-start(bf16[1024,16,256]{2,0,1:T(8,128)(2,1)} %bitcast.20), calls=%async_computation | async-start | bytes 16777216 | tf_op jit(solution)/shard_map/all_to_all | solution.py:33
  23.5 0.0 copy-done.2
  23.5 0.0 copy-done.3
  23.5 191.0 %all_gather.6 = s32[16384]{0:T(1024)S(1)} all-gather(s32[1024]{0:T(1024)S(1)} %add_select_fusion), channel_id=1, replica_groups=mesh['batch'=16,'gene'=2] {'batch'}, dimensions={0}, use_global_device_ids=true | all-gather | bytes 69632 | tf_op jit(solution)/shard_map/all_gather | solution.py:34
  214.5 0.0 copy-done.1
  214.6 18.3 %all_gather.7 = bf16[128,2048]{1,0:T(8,128)(2,1)} all-gather(bf16[128,128]{1,0:T(8,128)(2,1)S(1)} %multiply_convert_fusion.2), channel_id=1, replica_groups=mesh['batch'=16,'gene'=2] {'batch'}, dimensions={1}, use_global_device_ids=true | all-gather | bytes 557056 | tf_op jit(solution)/shard_map/all_gather | solution.py:59
  232.9 0.0 all-to-all-done
  232.9 57.8 %while.14 = (s32[]{:T(128)}, f32[256,3072]{1,0:T(8,128)S(1)}, bf16[16384,256]{1,0:T(8,128)(2,1)}, s32[16384]{0:T(1024)S(1)}, s32[]{:T(128)}, /*index=5*/s32[]{:T(128)}, s32[]{:T(128)}, s32[]{:T(128)}) while((s32[]{:T(128)}, f32[256,3072]{1,0:T(8,128)S(1)}, bf16[16384,256]{1,0:T(8,128)(2,1)}, s32[16384]{0:T(1024)S(1)}, s32[]{:T(128)}, ...), condition=%wide.region_1.2_spmd.clone, body=%wide.region_0.1_spmd.clone.sunk | while | flops 6456606720 | bytes 8437917 | solution.py:46
  232.9 14.4 %fusion.11 = f32[256,3072]{1,0:T(8,128)S(1)} fusion(s32[4096]{0:T(1024)S(1)} %dynamic_slice.21, f32[256,3072]{1,0:T(8,128)S(1)} %get-tuple-element.142, bf16[16384,256]{1,0:T(8,128)(2,1)} %get-tuple-element.151, s32[]{:T(128)S(6)} %select_n.16, pred[]{:T(512)S(6)} %compare.3), kind=kOutput, calls=%fused_computation.3.clone.1 | convolution fusion | flops 6456606720 | bytes 8404997 | tf_op jit(solution)/shard_map/while/body/eval_jaxpr/dot_general | solution.py:42
  247.4 14.4 %fusion.11 = f32[256,3072]{1,0:T(8,128)S(1)} fusion(s32[4096]{0:T(1024)S(1)} %dynamic_slice.21, f32[256,3072]{1,0:T(8,128)S(1)} %get-tuple-element.142, bf16[16384,256]{1,0:T(8,128)(2,1)} %get-tuple-element.151, s32[]{:T(128)S(6)} %select_n.16, pred[]{:T(512)S(6)} %compare.3), kind=kOutput, calls=%fused_computation.3.clone.1 | convolution fusion | flops 6456606720 | bytes 8404997 | tf_op jit(solution)/shard_map/while/body/eval_jaxpr/dot_general | solution.py:42
  261.8 14.4 %fusion.11 = f32[256,3072]{1,0:T(8,128)S(1)} fusion(s32[4096]{0:T(1024)S(1)} %dynamic_slice.21, f32[256,3072]{1,0:T(8,128)S(1)} %get-tuple-element.142, bf16[16384,256]{1,0:T(8,128)(2,1)} %get-tuple-element.151, s32[]{:T(128)S(6)} %select_n.16, pred[]{:T(512)S(6)} %compare.3), kind=kOutput, calls=%fused_computation.3.clone.1 | convolution fusion | flops 6456606720 | bytes 8404997 | tf_op jit(solution)/shard_map/while/body/eval_jaxpr/dot_general | solution.py:42
  276.3 14.4 %fusion.11 = f32[256,3072]{1,0:T(8,128)S(1)} fusion(s32[4096]{0:T(1024)S(1)} %dynamic_slice.21, f32[256,3072]{1,0:T(8,128)S(1)} %get-tuple-element.142, bf16[16384,256]{1,0:T(8,128)(2,1)} %get-tuple-element.151, s32[]{:T(128)S(6)} %select_n.16, pred[]{:T(512)S(6)} %compare.3), kind=kOutput, calls=%fused_computation.3.clone.1 | convolution fusion | flops 6456606720 | bytes 8404997 | tf_op jit(solution)/shard_map/while/body/eval_jaxpr/dot_general | solution.py:42
  290.7 2.5 copy.12
  293.3 0.2 reduce_sum.45
  293.4 44.2 %psum.7 = f32[3072]{0:T(1024)S(1)} all-reduce(f32[3072]{0:T(1024)S(1)} %reduce_sum.45), channel_id=1, replica_groups=mesh['batch'=16,'gene'=2] {'batch','gene'}, use_global_device_ids=true, to_apply=%region_3.4 | all-reduce | flops 3072 | bytes 24576 | tf_op jit(solution)/shard_map/psum | solution.py:50
  337.7 3.1 divide_log-plus-one_fusion
  340.8 0.2 reduce_sum.46
  341.1 0.4 multiply_reduce_fusion
  341.5 1.6 fusion.5
  343.1 0.0 copy-start
  343.1 2.0 copy.13
  345.0 0.0 copy-done
  345.0 12.4 %multiply_convert_fusion = bf16[6144,2048]{1,0:T(8,128)(2,1)} fusion(bf16[6144,128]{1,0:T(8,128)(2,1)S(1)} %bitcast.21, bf16[128,2048]{1,0:T(8,128)(2,1)S(1)} %copy-done), kind=kOutput, calls=%fused_computation.6 | convolution fusion | flops 3246391296 | bytes 27262976 | tf_op jit(solution)/shard_map/dot_general | solution.py:60
  (14 shorter events, 0.2 us)
Async XLA Ops:
  16.5 7.0 %copy-start.2 = (s32[1024]{0:T(1024)S(1)}, s32[1024]{0:T(1024)}, u32[]{:S(2)}) copy-start(s32[1024]{0:T(1024)} %param.8) | copy-start | bytes 12292
  16.5 7.0 %copy-start.3 = (s32[1024]{0:T(1024)S(1)}, s32[1024]{0:T(1024)}, u32[]{:S(2)}) copy-start(s32[1024]{0:T(1024)} %param.9) | copy-start | bytes 12292
  16.5 198.0 %copy-start.1 = (s32[128,128]{1,0:T(8,128)S(1)}, s32[128,128]{1,0:T(8,128)}, u32[]{:S(2)}) copy-start(s32[128,128]{1,0:T(8,128)} %param.11) | copy-start | bytes 196612
  16.5 216.4 %all-to-all-start = ((bf16[1024,16,256]{2,0,1:T(8,128)(2,1)}), bf16[1024,16,256]{2,0,1:T(8,128)(2,1)}, u32[]{:S(2)}, u32[]{:S(2)}) async-start(bf16[1024,16,256]{2,0,1:T(8,128)(2,1)} %bitcast.20), calls=%async_computation | async-start | bytes 16777216 | tf_op jit(solution)/shard_map/all_to_all | solution.py:33
  343.1 2.0 copy-start
where the time goes:
time: 358 us; the launch traced here: 357 us
  blocking collectives  253 us (71%)
  matrix products  70 us (20%)
  other arithmetic  14.7 us (4%)
  local copies, waits for them, and re-layouts  12 us (3%)
  starting transfers between devices  6.37 us (2%)
    all_gather x1, blocking collectives, on_device(): all_groups = lax.all_gather(cell_group, 'batch', axis=0, tiled=True)  191 us
    dot_general x4, matrix products, add_block(): lax.dot_general(block_counts, table, (((0,), (0,)), ((), ())), preferred_...  57.6 us
    psum x1, blocking collectives, on_device(): library = jnp.maximum(lax.psum(partial_library, ('batch', 'gene')), 1.0)  44.2 us
    all_gather x1, blocking collectives, on_device(): geno_piece = lax.all_gather(geno_local, 'batch', axis=1, tiled=True)  18.3 us
    dot_general x1, matrix products, on_device(): jnp.dot(standard_rows, geno_piece, preferred_element_type=jnp.float32)  12.4 us
    convert_element_type x1, other arithmetic, on_device(): rounded = umi_counts.astype(jnp.bfloat16)  9.05 us
    all_to_all x1, local copies, waits for them, and re-layouts, on_device(): lax.all_to_all(rounded, 'batch', split_axis=1, concat_axis=0, tiled=True)  7.43 us
  transfers between devices with their start and end apart: 1, of which 0 were waited for; matrix products, arithmetic and copies ran while one was open for 0% of the time, Pallas kernels for 0%

commit v1 on v0

--- a/solution.py
+++ b/solution.py
@@ -5,6 +5,11 @@
 
 TYPES = 24
 DONORS = 128
+
+
+def axis_by_axis(value, one, other):
+    partial = lax.psum(value, one)
+    return lax.psum(partial, other)
 
 
 def one_hot_rows(group_ids, total_groups):
@@ -47,7 +52,7 @@
         0, block_turns, add_block, jnp.zeros((genes_local, total_groups), jnp.float32)
     )
     partial_library = jnp.sum(pseudo, axis=0)
-    library = jnp.maximum(lax.psum(partial_library, ("batch", "gene")), 1.0)
+    library = jnp.maximum(axis_by_axis(partial_library, "gene", "batch"), 1.0)
     logged = jnp.log1p(10000.0 * pseudo / library[None, :]).reshape(genes_local, TYPES, DONORS)
     centred = logged - jnp.mean(logged, axis=2, keepdims=True)
     standard = (

time: 358 us -> 386 us (1.078)
  the two profiles are of different devices: /device:TPU:14 before, /device:TPU:0 now
where the time goes in v1:
time: 386 us; the launch traced here: 385 us
  blocking collectives  280 us (73%)
  matrix products  70 us (18%)
  other arithmetic  14.7 us (4%)
  local copies, waits for them, and re-layouts  12 us (3%)
  starting transfers between devices  7.6 us (2%)
    all_gather x1, blocking collectives, on_device(): all_groups = lax.all_gather(cell_group, 'batch', axis=0, tiled=True)  151 us
    all_gather x1, blocking collectives, on_device(): geno_piece = lax.all_gather(geno_local, 'batch', axis=1, tiled=True)  63.4 us
    dot_general x4, matrix products, add_block(): lax.dot_general(block_counts, table, (((0,), (0,)), ((), ())), preferred_...  57.6 us
    psum x1, blocking collectives, axis_by_axis(): return lax.psum(partial, other)  57.6 us
    dot_general x1, matrix products, on_device(): jnp.dot(standard_rows, geno_piece, preferred_element_type=jnp.float32)  12.4 us
    convert_element_type x1, other arithmetic, on_device(): rounded = umi_counts.astype(jnp.bfloat16)  9.05 us
    psum x1, blocking collectives, axis_by_axis(): partial = lax.psum(value, one)  8.07 us
  transfers between devices with their start and end apart: 1, of which 0 were waited for; matrix products, arithmetic and copies ran while one was open for 0% of the time, Pallas kernels for 0%

profile of v1, /device:TPU:0, one launch (start us, length us, event | category | flops | bytes accessed | tf_op | source)
XLA Modules:
  0.0 385.5 jit_solution(17358757050728967967)
XLA Ops:
  0.0 9.0 %convert_element_type.21 = bf16[1024,4096]{1,0:T(8,128)(2,1)} convert(s32[1024,4096]{1,0:T(8,128)} %param.7) | non-fusion elementwise | flops 4194304 | bytes 25165824 | tf_op jit(solution)/shard_map/convert_element_type | solution.py:37
  9.0 7.4 %copy.16 = bf16[128,16,8,256]{3,2,0,1:T(8,128)(2,1)} copy(bf16[128,16,8,256]{3,2,1,0:T(8,128)(2,1)} %bitcast.19) | data formatting | bytes 16777216 | tf_op jit(solution)/shard_map/all_to_all | solution.py:38
  16.5 0.0 copy-start.2
  16.5 0.0 copy-start.3
  16.5 0.0 copy-start.1
  16.5 7.6 %all-to-all-start = ((bf16[1024,16,256]{2,0,1:T(8,128)(2,1)}), bf16[1024,16,256]{2,0,1:T(8,128)(2,1)}, u32[]{:S(2)}, u32[]{:S(2)}) async-start(bf16[1024,16,256]{2,0,1:T(8,128)(2,1)} %bitcast.20), calls=%async_computation | async-start | bytes 16777216 | tf_op jit(solution)/shard_map/all_to_all | solution.py:38
  24.7 0.0 copy-done.2
  24.8 0.0 copy-done.3
  24.8 151.2 %all_gather.6 = s32[16384]{0:T(1024)S(1)} all-gather(s32[1024]{0:T(1024)S(1)} %add_select_fusion), channel_id=1, replica_groups=mesh['batch'=16,'gene'=2] {'batch'}, dimensions={0}, use_global_device_ids=true | all-gather | bytes 69632 | tf_op jit(solution)/shard_map/all_gather | solution.py:39
  176.0 0.0 copy-done.1
  176.1 63.4 %all_gather.7 = bf16[128,2048]{1,0:T(8,128)(2,1)} all-gather(bf16[128,128]{1,0:T(8,128)(2,1)S(1)} %multiply_convert_fusion.2), channel_id=1, replica_groups=mesh['batch'=16,'gene'=2] {'batch'}, dimensions={1}, use_global_device_ids=true | all-gather | bytes 557056 | tf_op jit(solution)/shard_map/all_gather | solution.py:64
  239.6 0.0 all-to-all-done
  239.6 57.8 %while.14 = (s32[]{:T(128)}, f32[256,3072]{1,0:T(8,128)S(1)}, bf16[16384,256]{1,0:T(8,128)(2,1)}, s32[16384]{0:T(1024)S(1)}, s32[]{:T(128)}, /*index=5*/s32[]{:T(128)}, s32[]{:T(128)}, s32[]{:T(128)}) while((s32[]{:T(128)}, f32[256,3072]{1,0:T(8,128)S(1)}, bf16[16384,256]{1,0:T(8,128)(2,1)}, s32[16384]{0:T(1024)S(1)}, s32[]{:T(128)}, ...), condition=%wide.region_1.2_spmd.clone, body=%wide.region_0.1_spmd.clone.sunk | while | flops 6456606720 | bytes 8437917 | solution.py:51
  239.6 14.4 %fusion.11 = f32[256,3072]{1,0:T(8,128)S(1)} fusion(s32[4096]{0:T(1024)S(1)} %dynamic_slice.21, f32[256,3072]{1,0:T(8,128)S(1)} %get-tuple-element.142, bf16[16384,256]{1,0:T(8,128)(2,1)} %get-tuple-element.151, s32[]{:T(128)S(6)} %select_n.16, pred[]{:T(512)S(6)} %compare.3), kind=kOutput, calls=%fused_computation.3.clone.1 | convolution fusion | flops 6456606720 | bytes 8404997 | tf_op jit(solution)/shard_map/while/body/eval_jaxpr/dot_general | solution.py:47
  254.0 14.4 %fusion.11 = f32[256,3072]{1,0:T(8,128)S(1)} fusion(s32[4096]{0:T(1024)S(1)} %dynamic_slice.21, f32[256,3072]{1,0:T(8,128)S(1)} %get-tuple-element.142, bf16[16384,256]{1,0:T(8,128)(2,1)} %get-tuple-element.151, s32[]{:T(128)S(6)} %select_n.16, pred[]{:T(512)S(6)} %compare.3), kind=kOutput, calls=%fused_computation.3.clone.1 | convolution fusion | flops 6456606720 | bytes 8404997 | tf_op jit(solution)/shard_map/while/body/eval_jaxpr/dot_general | solution.py:47
  268.5 14.4 %fusion.11 = f32[256,3072]{1,0:T(8,128)S(1)} fusion(s32[4096]{0:T(1024)S(1)} %dynamic_slice.21, f32[256,3072]{1,0:T(8,128)S(1)} %get-tuple-element.142, bf16[16384,256]{1,0:T(8,128)(2,1)} %get-tuple-element.151, s32[]{:T(128)S(6)} %select_n.16, pred[]{:T(512)S(6)} %compare.3), kind=kOutput, calls=%fused_computation.3.clone.1 | convolution fusion | flops 6456606720 | bytes 8404997 | tf_op jit(solution)/shard_map/while/body/eval_jaxpr/dot_general | solution.py:47
  282.9 14.4 %fusion.11 = f32[256,3072]{1,0:T(8,128)S(1)} fusion(s32[4096]{0:T(1024)S(1)} %dynamic_slice.21, f32[256,3072]{1,0:T(8,128)S(1)} %get-tuple-element.142, bf16[16384,256]{1,0:T(8,128)(2,1)} %get-tuple-element.151, s32[]{:T(128)S(6)} %select_n.16, pred[]{:T(512)S(6)} %compare.3), kind=kOutput, calls=%fused_computation.3.clone.1 | convolution fusion | flops 6456606720 | bytes 8404997 | tf_op jit(solution)/shard_map/while/body/eval_jaxpr/dot_general | solution.py:47
  297.4 2.5 copy.12
  299.9 0.2 reduce_sum.45
  300.1 8.1 %psum.14 = f32[3072]{0:T(1024)S(1)} all-reduce(f32[3072]{0:T(1024)S(1)} %reduce_sum.45), channel_id=1, replica_groups=mesh['batch'=16,'gene'=2] {'gene'}, use_global_device_ids=true, to_apply=%region_3.4 | all-reduce | flops 3072 | bytes 24576 | tf_op jit(solution)/shard_map/psum | solution.py:11
  308.1 57.6 %psum.15 = f32[3072]{0:T(1024)S(1)} all-reduce(f32[3072]{0:T(1024)S(1)} %psum.14), channel_id=1, replica_groups=mesh['batch'=16,'gene'=2] {'batch'}, use_global_device_ids=true, to_apply=%region_4.5 | all-reduce | flops 3072 | bytes 24576 | tf_op jit(solution)/shard_map/psum | solution.py:12
  365.8 3.1 divide_log-plus-one_fusion
  368.9 0.2 reduce_sum.46
  369.1 0.4 multiply_reduce_fusion
  369.6 1.6 fusion.5
  371.1 0.0 copy-start
  371.2 2.0 copy.13
  373.1 0.0 copy-done
  373.1 12.4 %multiply_convert_fusion = bf16[6144,2048]{1,0:T(8,128)(2,1)} fusion(bf16[6144,128]{1,0:T(8,128)(2,1)S(1)} %bitcast.21, bf16[128,2048]{1,0:T(8,128)(2,1)S(1)} %copy-done), kind=kOutput, calls=%fused_computation.6 | convolution fusion | flops 3246391296 | bytes 27262976 | tf_op jit(solution)/shard_map/dot_general | solution.py:65
  (14 shorter events, 0.2 us)
Async XLA Ops:
  16.5 8.3 %copy-start.2 = (s32[1024]{0:T(1024)S(1)}, s32[1024]{0:T(1024)}, u32[]{:S(2)}) copy-start(s32[1024]{0:T(1024)} %param.8) | copy-start | bytes 12292
  16.5 8.3 %copy-start.3 = (s32[1024]{0:T(1024)S(1)}, s32[1024]{0:T(1024)}, u32[]{:S(2)}) copy-start(s32[1024]{0:T(1024)} %param.9) | copy-start | bytes 12292
  16.5 159.5 %copy-start.1 = (s32[128,128]{1,0:T(8,128)S(1)}, s32[128,128]{1,0:T(8,128)}, u32[]{:S(2)}) copy-start(s32[128,128]{1,0:T(8,128)} %param.11) | copy-start | bytes 196612
  16.5 223.1 %all-to-all-start = ((bf16[1024,16,256]{2,0,1:T(8,128)(2,1)}), bf16[1024,16,256]{2,0,1:T(8,128)(2,1)}, u32[]{:S(2)}, u32[]{:S(2)}) async-start(bf16[1024,16,256]{2,0,1:T(8,128)(2,1)} %bitcast.20), calls=%async_computation | async-start | bytes 16777216 | tf_op jit(solution)/shard_map/all_to_all | solution.py:38
  371.1 2.0 copy-start
